TPU v7x, 32 devices: a whole 2x2x4 slice. The times are simulated.
32 devices in a mesh: gx: 4 (over x, core), gy: 8 (over z, y).
Axes of the slice: x: 2, y: 2, z: 4, core: 2. Of those that a mesh axis runs over, the one named last changes fastest.
Arguments:
- populations: float32 [19, 32, 64, 128], P(None, 'gx', 'gy'), may hold values from 0 to 1, as said below
- cell_kind: int32 [32, 64, 128], P('gx', 'gy'), may hold values from 0 to 3, as said below
- outlet_region: int32 [32, 64], P('gx', 'gy'), may hold values from 0 to 63, as said below
Outputs:
- final_populations: float32 [19, 32, 64, 128], P(None, 'gx', 'gy')
- outlet_means: float32 [2, 64], replicated
Inputs may be any that keep to these rules, and one draw needn't show every extreme that they name: `populations`: positive. `cell_kind`: the plane z = 0 is all inlet (2), the plane z = 127 all outlet (3); all other cells are fluid (0) or wall (1). `outlet_region`: every region names at least one column; ids are constant on aligned tiles of 4 x 4 columns.
All inputs are finite; a program needn't handle non-finite values.
Results may differ from a plain program's by a relative error of at most 0.0001.
Values sent between devices are 32-bit elements; how exact they have to be, the bound alone decides.
A program may use at most 64 MiB of HBM per device.

v0:
```python
import jax
import jax.numpy as jnp
from jax import lax
from jax.sharding import PartitionSpec as P

REGIONS = 64
STEPS = 2
VELOCITIES = (
    (0, 0, 0),
    (1, 0, 0),
    (-1, 0, 0),
    (0, 1, 0),
    (0, -1, 0),
    (0, 0, 1),
    (0, 0, -1),
    (1, 1, 0),
    (-1, -1, 0),
    (1, -1, 0),
    (-1, 1, 0),
    (1, 0, 1),
    (-1, 0, -1),
    (1, 0, -1),
    (-1, 0, 1),
    (0, 1, 1),
    (0, -1, -1),
    (0, 1, -1),
    (0, -1, 1),
)
WEIGHTS = (1.0 / 3.0,) + (1.0 / 18.0,) * 6 + (1.0 / 36.0,) * 12
OPPOSITE = (0, 2, 1, 4, 3, 6, 5, 8, 7, 10, 9, 12, 11, 14, 13, 16, 15, 18, 17)
RELAX_TIME = 0.8
INLET_SPEED = 0.05
RISING_X = (1, 7, 9, 11, 13)
FALLING_X = (2, 8, 10, 12, 14)
RISING_Y = (3, 7, 10, 15, 17)
FALLING_Y = (4, 8, 9, 16, 18)


def from_behind(block, axis, distance):
    devices = range(lax.axis_size(axis))
    route = [(i - distance, i) for i in devices if i - distance in devices]
    return lax.ppermute(block, axis, route)


def from_behind_2(value, axis, steps):
    count = lax.axis_size(axis)
    pairs = [(source, (source + steps) % count) for source in range(count)]
    return lax.ppermute(value, axis, pairs)


def momentum(current, direction):
    total = jnp.zeros_like(current[0])
    for number in range(19):
        factor = VELOCITIES[number][direction]
        if factor != 0:
            total = total + factor * current[number]
    return total


def equilibrium(density, vel_x, vel_y, vel_z):
    speed_sq = vel_x * vel_x + vel_y * vel_y + vel_z * vel_z
    result = []
    for number in range(19):
        comp_x, comp_y, comp_z = VELOCITIES[number]
        projected = comp_x * vel_x + comp_y * vel_y + comp_z * vel_z
        result.append(
            WEIGHTS[number]
            * density
            * (1.0 + 3.0 * projected + 4.5 * projected * projected - 1.5 * speed_sq)
        )
    return jnp.stack(result)


def collide(current, kinds, col_mean):
    density = jnp.sum(current, axis=0)
    vel_x = momentum(current, 0) / density
    vel_y = momentum(current, 1) / density
    vel_z = momentum(current, 2) / density
    relaxed = current - (current - equilibrium(density, vel_x, vel_y, vel_z)) / RELAX_TIME
    bounced = jnp.stack([current[OPPOSITE[number]] for number in range(19)])
    unity = jnp.ones_like(density)
    still = jnp.zeros_like(density)
    inlet = equilibrium(unity, still, still, INLET_SPEED * unity)
    outlet = equilibrium(col_mean * unity, vel_x, vel_y, vel_z)
    post = jnp.where(kinds == 1, bounced, relaxed)
    post = jnp.where(kinds == 2, inlet, post)
    post = jnp.where(kinds == 3, outlet, post)
    return post


def stream(padded, rows_x, rows_y):
    moved = []
    for number in range(19):
        comp_x, comp_y, comp_z = VELOCITIES[number]
        plane = padded[
            number, 1 - comp_x : 1 - comp_x + rows_x, 1 - comp_y : 1 - comp_y + rows_y, :
        ]
        moved.append(jnp.roll(plane, comp_z, axis=2))
    return jnp.stack(moved)


def outlet_mean(current, kinds, onehot):
    density = jnp.sum(current, axis=0)
    is_outlet = kinds == 3
    column = jnp.sum(jnp.where(is_outlet, density, 0.0), axis=2).reshape(-1)
    col_count = jnp.sum(is_outlet.astype(jnp.float32), axis=2).reshape(-1)
    local_sums = jnp.dot(onehot, column, precision=lax.Precision.HIGHEST)
    local_counts = jnp.dot(onehot, col_count, precision=lax.Precision.HIGHEST)
    totals, counts = lax.psum((local_sums, local_counts), ("gx", "gy"))
    return totals / counts


def widen_first(post, from_lower, from_upper):
    blank = jnp.zeros_like(post[0, :1])
    planes = []
    for number in range(19):
        lower = from_lower[RISING_X.index(number)][None] if number in RISING_X else blank
        upper = from_upper[FALLING_X.index(number)][None] if number in FALLING_X else blank
        planes.append(jnp.concatenate([lower, post[number], upper], axis=0))
    return planes


def widen_second(planes, from_lower, from_upper):
    blank = jnp.zeros_like(planes[0][:, :1])
    padded = []
    for number in range(19):
        lower = from_lower[RISING_Y.index(number)][:, None] if number in RISING_Y else blank
        upper = from_upper[FALLING_Y.index(number)][:, None] if number in FALLING_Y else blank
        padded.append(jnp.concatenate([lower, planes[number], upper], axis=1))
    return jnp.stack(padded)


def body(populations, cell_kind, outlet_region):
    cells_x = populations.shape[1]
    cells_y = populations.shape[2]
    labels = jnp.arange(REGIONS, dtype=jnp.int32)
    onehot = (outlet_region.reshape(-1)[None, :] == labels[:, None]).astype(jnp.float32)
    current = populations
    means = []
    for timestep in range(STEPS):
        region_mean = outlet_mean(current, cell_kind, onehot)
        means.append(region_mean)
        col_mean = jnp.dot(region_mean, onehot, precision=lax.Precision.HIGHEST).reshape(
            cells_x, cells_y
        )[:, :, None]
        post = collide(current, cell_kind, col_mean)
        lower_x = from_behind(jnp.stack([post[number, -1] for number in RISING_X]), "gx", 1)
        upper_x = from_behind(jnp.stack([post[number, 0] for number in FALLING_X]), "gx", -1)
        planes = widen_first(post, lower_x, upper_x)
        lower_y = from_behind_2(jnp.stack([planes[number][:, -1] for number in RISING_Y]), "gy", 1)
        upper_y = from_behind_2(jnp.stack([planes[number][:, 0] for number in FALLING_Y]), "gy", -1)
        padded = widen_second(planes, lower_y, upper_y)
        current = stream(padded, cells_x, cells_y)
    return (current, jnp.stack(means))


def solution(mesh):
    in_specs = (P(None, "gx", "gy", None), P("gx", "gy", None), P("gx", "gy"))
    out_specs = (P(None, "gx", "gy", None), P())
    return jax.shard_map(body, mesh=mesh, in_specs=in_specs, out_specs=out_specs, check_vma=False)
```

profile of v0, /device:TPU:1, one launch (start us, length us, event | category | flops | bytes accessed | tf_op | source)
XLA Modules:
  0.0 127.7 jit_solution(15017054482665278097)
XLA Ops:
  0.7 0.8 constant_dynamic-update-slice_fusion.47
  1.5 1.1 reduce_sum.854
  2.6 0.1 constant_dynamic-update-slice_fusion.66
  2.7 0.7 copy-done.1
  3.4 0.1 convert_reduce_fusion
  4.0 0.1 reshape.1611
  4.1 0.6 copy-done.2
  4.7 0.1 eq.30
  4.7 0.1 reshape.1609
  4.8 0.1 convolution_bitcast_fusion.3
  4.9 0.2 convolution_bitcast_fusion.4
  5.1 40.5 %all-reduce = (f32[64]{0:T(128)S(1)}, f32[64]{0:T(128)S(1)}) all-reduce(f32[64]{0:T(128)S(1)} %convolution_bitcast_fusion.4, f32[64]{0:T(128)S(1)} %convolution_bitcast_fusion.3), channel_id=1, replica_groups=mesh['gx'=4,'gy'=8] {'gx','gy'}, use_global_device_ids=true, to_apply=%region_2.3 | all-reduce | flops 128 | bytes 1024 | tf_op jit(solution)/shard_map/psum | solution.py:109
  45.6 0.1 broadcast_multiply_fusion.2
  45.7 0.1 mul.2993
  45.8 0.1 mul.3019
  45.9 0.1 mul.3049
  46.3 0.1 constant_dynamic-update-slice_fusion.48
  46.6 0.1 constant_dynamic-update-slice_fusion.14
  46.7 0.1 constant_dynamic-update-slice_fusion.13
  46.8 0.1 constant_dynamic-update-slice_fusion.12
  46.9 0.1 constant_dynamic-update-slice_fusion.11
  46.9 0.1 constant_dynamic-update-slice_fusion.10
  47.2 0.1 constant_dynamic-update-slice_fusion.7
  47.2 0.1 constant_dynamic-update-slice_fusion.6
  47.3 0.1 constant_dynamic-update-slice_fusion.5
  47.4 0.1 constant_dynamic-update-slice_fusion.4
  47.5 0.1 constant_dynamic-update-slice_fusion.3
  47.8 0.3 select_select_fusion.1
  48.2 5.3 %collective-permute-start = (f32[5,8,128]{2,1,0:T(8,128)S(1)}, f32[5,8,128]{2,1,0:T(8,128)S(1)}, u32[]{:S(2)}, u32[]{:S(2)}) collective-permute-start(f32[5,8,128]{2,1,0:T(8,128)S(1)} %get-tuple-element.153), channel_id=1, source_target_pairs={{0,8},{8,16},{16,24},{1,9},{9,17},{17,25},{2,10},{10,18},{18,26},{... | collective-permute-start | bytes 61448 | tf_op jit(solution)/shard_map/ppermute | solution.py:42
  53.5 1.9 %collective-permute-start.1 = (f32[5,8,128]{2,1,0:T(8,128)S(1)}, f32[5,8,128]{2,1,0:T(8,128)S(1)}, u32[]{:S(2)}, u32[]{:S(2)}) collective-permute-start(f32[5,8,128]{2,1,0:T(8,128)S(1)} %get-tuple-element.154), channel_id=1, source_target_pairs={{8,0},{16,8},{24,16},{9,1},{17,9},{25,17},{10,2},{18,10},{26,18},{... | collective-permute-start | bytes 61448 | tf_op jit(solution)/shard_map/ppermute | solution.py:42
  55.5 3.1 %collective-permute-done.1 = f32[5,8,128]{2,1,0:T(8,128)S(1)} collective-permute-done((f32[5,8,128]{2,1,0:T(8,128)S(1)}, f32[5,8,128]{2,1,0:T(8,128)S(1)}, u32[]{:S(2)}, u32[]{:S(2)}) %collective-permute-start.1) | collective-permute-done | bytes 20512 | tf_op jit(solution)/shard_map/ppermute | solution.py:42
  58.7 0.3 collective-permute-start.2
  59.2 4.0 %collective-permute-start.3 = (f32[5,10,128]{2,0,1:T(8,128)S(1)}, f32[5,10,128]{2,0,1:T(8,128)S(1)}, u32[]{:S(2)}, u32[]{:S(2)}) collective-permute-start(f32[5,10,128]{2,0,1:T(8,128)S(1)} %stack.147), channel_id=1, source_target_pairs={{0,7},{1,0},{2,1},{3,2},{4,3},{5,4},{6,5},{7,6},{8,15},{9,8},{10,9... | collective-permute-start | bytes 76808 | tf_op jit(solution)/shard_map/ppermute | solution.py:48
  63.2 1.1 collective-permute-done.2
  65.7 0.3 constant_dynamic-update-slice_fusion.152
  66.8 0.1 fusion.168
  67.0 0.1 reshape.1615
  67.0 0.1 convolution_bitcast_fusion.1
  67.2 38.7 %psum.26 = f32[64]{0:T(128)S(1)} all-reduce(f32[64]{0:T(128)S(1)} %convolution_bitcast_fusion.1), channel_id=1, replica_groups=mesh['gx'=4,'gy'=8] {'gx','gy'}, use_global_device_ids=true, to_apply=%region_6.7 | all-reduce | flops 64 | bytes 512 | tf_op jit(solution)/shard_map/psum | solution.py:109
  105.9 0.1 broadcast_multiply_fusion.1
  106.0 0.1 mul.3122
  106.1 0.1 mul.3148
  106.2 0.1 mul.3178
  106.3 0.1 constant_dynamic-update-slice_fusion.94
  107.7 0.3 select_select_fusion
  108.2 5.3 %collective-permute-start.4 = (f32[5,8,128]{2,1,0:T(8,128)S(1)}, f32[5,8,128]{2,1,0:T(8,128)S(1)}, u32[]{:S(2)}, u32[]{:S(2)}) collective-permute-start(f32[5,8,128]{2,1,0:T(8,128)S(1)} %get-tuple-element.125), channel_id=1, source_target_pairs={{0,8},{8,16},{16,24},{1,9},{9,17},{17,25},{2,10},{10,18},{18,26},{... | collective-permute-start | bytes 61448 | tf_op jit(solution)/shard_map/ppermute | solution.py:42
  113.4 1.9 %collective-permute-start.5 = (f32[5,8,128]{2,1,0:T(8,128)S(1)}, f32[5,8,128]{2,1,0:T(8,128)S(1)}, u32[]{:S(2)}, u32[]{:S(2)}) collective-permute-start(f32[5,8,128]{2,1,0:T(8,128)S(1)} %get-tuple-element.124), channel_id=1, source_target_pairs={{8,0},{16,8},{24,16},{9,1},{17,9},{25,17},{10,2},{18,10},{26,18},{... | collective-permute-start | bytes 61448 | tf_op jit(solution)/shard_map/ppermute | solution.py:42
  115.4 0.6 pad_maximum_fusion.164
  116.0 2.6 %collective-permute-done.5 = f32[5,8,128]{2,1,0:T(8,128)S(1)} collective-permute-done((f32[5,8,128]{2,1,0:T(8,128)S(1)}, f32[5,8,128]{2,1,0:T(8,128)S(1)}, u32[]{:S(2)}, u32[]{:S(2)}) %collective-permute-start.5) | collective-permute-done | bytes 20512 | tf_op jit(solution)/shard_map/ppermute | solution.py:42
  118.7 0.8 collective-permute-start.7
  119.5 0.7 collective-permute-start.6
  120.6 0.1 slice.1047
  120.7 4.5 %collective-permute-done.6 = f32[5,10,128]{2,0,1:T(8,128)S(1)} collective-permute-done((f32[5,10,128]{2,0,1:T(8,128)S(1)}, f32[5,10,128]{2,0,1:T(8,128)S(1)}, u32[]{:S(2)}, u32[]{:S(2)}) %collective-permute-start.6) | collective-permute-done | bytes 25632 | tf_op jit(solution)/shard_map/ppermute | solution.py:48
  126.0 0.1 constant_dynamic-update-slice_fusion.176
  126.1 0.1 constant_dynamic-update-slice_fusion.175
  126.3 0.1 constant_dynamic-update-slice_fusion.170
  126.3 0.1 constant_dynamic-update-slice_fusion.169
  126.4 0.1 constant_dynamic-update-slice_fusion.168
  126.5 0.1 constant_dynamic-update-slice_fusion.167
  126.6 0.1 constant_dynamic-update-slice_fusion.166
  126.7 0.1 constant_dynamic-update-slice_fusion.165
  126.7 0.1 constant_dynamic-update-slice_fusion.164
  126.8 0.1 constant_dynamic-update-slice_fusion.163
  126.9 0.8 copy-done.3
  (231 shorter events, 5.9 us)
Async XLA Ops:
  0.6 2.0 %copy-start = (f32[19,8,8,128]{3,2,1,0:T(8,128)S(1)}, f32[19,8,8,128]{3,2,1,0:T(8,128)}, u32[]{:S(2)}) copy-start(f32[19,8,8,128]{3,2,1,0:T(8,128)} %param.3) | copy-start | bytes 1867780
  2.6 0.8 copy-start.1
  4.0 0.7 copy-start.2
  48.2 10.4 %collective-permute-start = (f32[5,8,128]{2,1,0:T(8,128)S(1)}, f32[5,8,128]{2,1,0:T(8,128)S(1)}, u32[]{:S(2)}, u32[]{:S(2)}) collective-permute-start(f32[5,8,128]{2,1,0:T(8,128)S(1)} %get-tuple-element.153), channel_id=1, source_target_pairs={{0,8},{8,16},{16,24},{1,9},{9,17},{17,25},{2,10},{10,18},{18,26},{... | collective-permute-start | bytes 61448 | tf_op jit(solution)/shard_map/ppermute | solution.py:42
  53.5 5.1 %collective-permute-start.1 = (f32[5,8,128]{2,1,0:T(8,128)S(1)}, f32[5,8,128]{2,1,0:T(8,128)S(1)}, u32[]{:S(2)}, u32[]{:S(2)}) collective-permute-start(f32[5,8,128]{2,1,0:T(8,128)S(1)} %get-tuple-element.154), channel_id=1, source_target_pairs={{8,0},{16,8},{24,16},{9,1},{17,9},{25,17},{10,2},{18,10},{26,18},{... | collective-permute-start | bytes 61448 | tf_op jit(solution)/shard_map/ppermute | solution.py:42
  58.7 5.6 %collective-permute-start.2 = (f32[5,10,128]{2,0,1:T(8,128)S(1)}, f32[5,10,128]{2,0,1:T(8,128)S(1)}, u32[]{:S(2)}, u32[]{:S(2)}) collective-permute-start(f32[5,10,128]{2,0,1:T(8,128)S(1)} %stack.145), channel_id=1, source_target_pairs={{0,1},{1,2},{2,3},{3,4},{4,5},{5,6},{6,7},{7,0},{8,9},{9,10},{10,1... | collective-permute-start | bytes 76808 | tf_op jit(solution)/shard_map/ppermute | solution.py:48
  59.2 5.2 %collective-permute-start.3 = (f32[5,10,128]{2,0,1:T(8,128)S(1)}, f32[5,10,128]{2,0,1:T(8,128)S(1)}, u32[]{:S(2)}, u32[]{:S(2)}) collective-permute-start(f32[5,10,128]{2,0,1:T(8,128)S(1)} %stack.147), channel_id=1, source_target_pairs={{0,7},{1,0},{2,1},{3,2},{4,3},{5,4},{6,5},{7,6},{8,15},{9,8},{10,9... | collective-permute-start | bytes 76808 | tf_op jit(solution)/shard_map/ppermute | solution.py:48
  108.2 7.8 %collective-permute-start.4 = (f32[5,8,128]{2,1,0:T(8,128)S(1)}, f32[5,8,128]{2,1,0:T(8,128)S(1)}, u32[]{:S(2)}, u32[]{:S(2)}) collective-permute-start(f32[5,8,128]{2,1,0:T(8,128)S(1)} %get-tuple-element.125), channel_id=1, source_target_pairs={{0,8},{8,16},{16,24},{1,9},{9,17},{17,25},{2,10},{10,18},{18,26},{... | collective-permute-start | bytes 61448 | tf_op jit(solution)/shard_map/ppermute | solution.py:42
  113.4 5.1 %collective-permute-start.5 = (f32[5,8,128]{2,1,0:T(8,128)S(1)}, f32[5,8,128]{2,1,0:T(8,128)S(1)}, u32[]{:S(2)}, u32[]{:S(2)}) collective-permute-start(f32[5,8,128]{2,1,0:T(8,128)S(1)} %get-tuple-element.124), channel_id=1, source_target_pairs={{8,0},{16,8},{24,16},{9,1},{17,9},{25,17},{10,2},{18,10},{26,18},{... | collective-permute-start | bytes 61448 | tf_op jit(solution)/shard_map/ppermute | solution.py:42
  118.7 6.9 %collective-permute-start.7 = (f32[5,10,128]{2,0,1:T(8,128)S(1)}, f32[5,10,128]{2,0,1:T(8,128)S(1)}, u32[]{:S(2)}, u32[]{:S(2)}) collective-permute-start(f32[5,10,128]{2,0,1:T(8,128)S(1)} %stack.347), channel_id=1, source_target_pairs={{0,7},{1,0},{2,1},{3,2},{4,3},{5,4},{6,5},{7,6},{8,15},{9,8},{10,9... | collective-permute-start | bytes 76808 | tf_op jit(solution)/shard_map/ppermute | solution.py:48
  119.5 5.6 %collective-permute-start.6 = (f32[5,10,128]{2,0,1:T(8,128)S(1)}, f32[5,10,128]{2,0,1:T(8,128)S(1)}, u32[]{:S(2)}, u32[]{:S(2)}) collective-permute-start(f32[5,10,128]{2,0,1:T(8,128)S(1)} %stack.172), channel_id=1, source_target_pairs={{0,1},{1,2},{2,3},{3,4},{4,5},{5,6},{6,7},{7,0},{8,9},{9,10},{10,1... | collective-permute-start | bytes 76808 | tf_op jit(solution)/shard_map/ppermute | solution.py:48
  126.9 0.8 copy-start.3
where the time goes:
time: 128 us
  blocking collectives  79.2 us (62%)
  starting transfers between devices  20.2 us (16%)
  waiting for transfers between devices  11.3 us (9%)
  other arithmetic  8.05 us (6%)
  local copies, waits for them, and re-layouts  6.31 us (5%)
  between operations  2.01 us (2%)
    psum x2, blocking collectives, outlet_mean(): totals, counts = lax.psum((local_sums, local_counts), ('gx', 'gy'))  79.2 us
    ppermute x4, starting transfers between devices, from_behind(): return lax.ppermute(block, axis, route)  14.4 us
    ppermute x4, starting transfers between devices, from_behind_2(): return lax.ppermute(value, axis, pairs)  5.84 us
    ppermute x4, waiting for transfers between devices, from_behind(): return lax.ppermute(block, axis, route)  5.67 us
    ppermute x4, waiting for transfers between devices, from_behind_2(): return lax.ppermute(value, axis, pairs)  5.62 us
    unnamed x80, other arithmetic  4.53 us
    unnamed x79, local copies, waits for them, and re-layouts  3.4 us
  transfers between devices with their start and end apart: 8, of which 4 were waited for; matrix products, arithmetic and copies ran while one was open for 1% of the time, Pallas kernels for 0%

commit v1 on v0

--- a/solution.py
+++ b/solution.py
@@ -34,6 +34,11 @@
 FALLING_X = (2, 8, 10, 12, 14)
 RISING_Y = (3, 7, 10, 15, 17)
 FALLING_Y = (4, 8, 9, 16, 18)
+
+
+def axis_by_axis(array, axis_one, axis_two):
+    half = lax.psum(array, axis_one)
+    return lax.psum(half, axis_two)
 
 
 def from_behind(block, axis, distance):
@@ -106,7 +111,7 @@
     col_count = jnp.sum(is_outlet.astype(jnp.float32), axis=2).reshape(-1)
     local_sums = jnp.dot(onehot, column, precision=lax.Precision.HIGHEST)
     local_counts = jnp.dot(onehot, col_count, precision=lax.Precision.HIGHEST)
-    totals, counts = lax.psum((local_sums, local_counts), ("gx", "gy"))
+    totals, counts = axis_by_axis((local_sums, local_counts), "gy", "gx")
     return totals / counts
 
 

time: 128 us -> 100 us (0.78)
  blocking collectives: 79.2 us -> 55.1 us
  starting transfers between devices: 20.2 us -> 17.4 us
    psum x2 -> x4, blocking collectives: 79.2 us -> 55.1 us  [the longest x2 36.9 us: axis_by_axis(): half = lax.psum(array, axis_one)]
    ppermute x4, starting transfers between devices: 14.4 us -> 11.6 us  [from_behind(): return lax.ppermute(block, axis, route)]
  transfers between devices with their start and end apart: 8 -> 8, of which waited for: 4 -> 4; matrix products, arithmetic and copies ran while one was open for 1% -> 2% of each run, Pallas kernels for 0% -> 0%
where the time goes in v1:
time: 100 us
  blocking collectives  55.1 us (55%)
  starting transfers between devices  17.4 us (17%)
  waiting for transfers between devices  10.5 us (10%)
  other arithmetic  8.06 us (8%)
  local copies, waits for them, and re-layouts  6.31 us (6%)
  between operations  2.03 us (2%)
    psum x2, blocking collectives, axis_by_axis(): half = lax.psum(array, axis_one)  36.9 us
    psum x2, blocking collectives, axis_by_axis(): return lax.psum(half, axis_two)  18.2 us
    ppermute x4, starting transfers between devices, from_behind(): return lax.ppermute(block, axis, route)  11.6 us
    ppermute x4, starting transfers between devices, from_behind_2(): return lax.ppermute(value, axis, pairs)  5.81 us
    ppermute x4, waiting for transfers between devices, from_behind(): return lax.ppermute(block, axis, route)  5.67 us
    ppermute x4, waiting for transfers between devices, from_behind_2(): return lax.ppermute(value, axis, pairs)  4.86 us
    unnamed x80, other arithmetic  4.53 us
    unnamed x79, local copies, waits for them, and re-layouts  3.41 us
  transfers between devices with their start and end apart: 8, of which 4 were waited for; matrix products, arithmetic and copies ran while one was open for 2% of the time, Pallas kernels for 0%

profile of v1, /device:TPU:1, one launch (start us, length us, event | category | flops | bytes accessed | tf_op | source)
XLA Modules:
  0.0 100.1 jit_solution(11535391032427421951)
XLA Ops:
  0.7 0.8 constant_dynamic-update-slice_fusion.47
  1.5 1.1 %reduce_sum.854 = f32[8,8,128]{2,1,0:T(8,128)S(1)} reduce(f32[19,8,8,128]{3,2,1,0:T(8,128)} %param.3, f32[]{:T(128)} %constant.20.clone.1), dimensions={0}, to_apply=%region_0.0 | reduce | flops 147456 | bytes 655364 | tf_op jit(solution)/shard_map/reduce_sum | solution.py:108
  2.6 0.1 constant_dynamic-update-slice_fusion.66
  2.7 0.7 copy-done.1
  3.4 0.1 convert_reduce_fusion
  4.0 0.1 reshape.1611
  4.1 0.6 copy-done.2
  4.7 0.1 eq.30
  4.7 0.1 reshape.1609
  4.8 0.1 convolution_bitcast_fusion.3
  4.9 0.2 convolution_bitcast_fusion.4
  5.1 18.8 %all-reduce = (f32[64]{0:T(128)S(1)}, f32[64]{0:T(128)S(1)}) all-reduce(f32[64]{0:T(128)S(1)} %convolution_bitcast_fusion.4, f32[64]{0:T(128)S(1)} %convolution_bitcast_fusion.3), channel_id=1, replica_groups=mesh['gx'=4,'gy'=8] {'gy'}, use_global_device_ids=true, to_apply=%region_2.3 | all-reduce | flops 128 | bytes 1024 | tf_op jit(solution)/shard_map/psum | solution.py:40
  23.9 9.4 %all-reduce.1 = (f32[64]{0:T(128)S(1)}, f32[64]{0:T(128)S(1)}) all-reduce(f32[64]{0:T(128)S(1)} %get-tuple-element.6, f32[64]{0:T(128)S(1)} %get-tuple-element.7), channel_id=1, replica_groups=mesh['gx'=4,'gy'=8] {'gx'}, use_global_device_ids=true, to_apply=%region_3.4 | all-reduce | flops 128 | bytes 1024 | tf_op jit(solution)/shard_map/psum | solution.py:41
  33.3 0.1 broadcast_multiply_fusion.2
  33.4 0.1 mul.2993
  33.5 0.1 mul.3019
  33.6 0.1 mul.3049
  34.0 0.1 constant_dynamic-update-slice_fusion.48
  34.4 0.1 constant_dynamic-update-slice_fusion.13
  34.5 0.1 constant_dynamic-update-slice_fusion.12
  34.6 0.1 constant_dynamic-update-slice_fusion.11
  34.6 0.1 constant_dynamic-update-slice_fusion.10
  34.7 0.1 constant_dynamic-update-slice_fusion.9
  34.8 0.1 constant_dynamic-update-slice_fusion.8
  34.9 0.1 constant_dynamic-update-slice_fusion.7
  34.9 0.1 constant_dynamic-update-slice_fusion.6
  35.2 0.1 constant_dynamic-update-slice_fusion.3
  35.3 0.1 constant_dynamic-update-slice_fusion.2
  35.5 0.3 select_select_fusion.1
  35.9 3.9 %collective-permute-start = (f32[5,8,128]{2,1,0:T(8,128)S(1)}, f32[5,8,128]{2,1,0:T(8,128)S(1)}, u32[]{:S(2)}, u32[]{:S(2)}) collective-permute-start(f32[5,8,128]{2,1,0:T(8,128)S(1)} %get-tuple-element.155), channel_id=1, source_target_pairs={{0,8},{8,16},{16,24},{1,9},{9,17},{17,25},{2,10},{10,18},{18,26},{... | collective-permute-start | bytes 61448 | tf_op jit(solution)/shard_map/ppermute | solution.py:47
  39.8 1.9 %collective-permute-start.1 = (f32[5,8,128]{2,1,0:T(8,128)S(1)}, f32[5,8,128]{2,1,0:T(8,128)S(1)}, u32[]{:S(2)}, u32[]{:S(2)}) collective-permute-start(f32[5,8,128]{2,1,0:T(8,128)S(1)} %get-tuple-element.156), channel_id=1, source_target_pairs={{8,0},{16,8},{24,16},{9,1},{17,9},{25,17},{10,2},{18,10},{26,18},{... | collective-permute-start | bytes 61448 | tf_op jit(solution)/shard_map/ppermute | solution.py:47
  41.8 3.1 %collective-permute-done.1 = f32[5,8,128]{2,1,0:T(8,128)S(1)} collective-permute-done((f32[5,8,128]{2,1,0:T(8,128)S(1)}, f32[5,8,128]{2,1,0:T(8,128)S(1)}, u32[]{:S(2)}, u32[]{:S(2)}) %collective-permute-start.1) | collective-permute-done | bytes 20512 | tf_op jit(solution)/shard_map/ppermute | solution.py:47
  45.3 4.2 %collective-permute-start.3 = (f32[5,10,128]{2,0,1:T(8,128)S(1)}, f32[5,10,128]{2,0,1:T(8,128)S(1)}, u32[]{:S(2)}, u32[]{:S(2)}) collective-permute-start(f32[5,10,128]{2,0,1:T(8,128)S(1)} %stack.147), channel_id=1, source_target_pairs={{0,7},{1,0},{2,1},{3,2},{4,3},{5,4},{6,5},{7,6},{8,15},{9,8},{10,9... | collective-permute-start | bytes 76808 | tf_op jit(solution)/shard_map/ppermute | solution.py:53
  49.5 1.1 %collective-permute-done.2 = f32[5,10,128]{2,0,1:T(8,128)S(1)} collective-permute-done((f32[5,10,128]{2,0,1:T(8,128)S(1)}, f32[5,10,128]{2,0,1:T(8,128)S(1)}, u32[]{:S(2)}, u32[]{:S(2)}) %collective-permute-start.2) | collective-permute-done | bytes 25632 | tf_op jit(solution)/shard_map/ppermute | solution.py:53
  52.0 0.3 constant_dynamic-update-slice_fusion.152
  53.2 0.1 fusion.168
  53.3 0.1 reshape.1615
  53.4 0.1 convolution_bitcast_fusion.1
  53.5 18.1 %psum.52 = f32[64]{0:T(128)S(1)} all-reduce(f32[64]{0:T(128)S(1)} %convolution_bitcast_fusion.1), channel_id=1, replica_groups=mesh['gx'=4,'gy'=8] {'gy'}, use_global_device_ids=true, to_apply=%region_8.9 | all-reduce | flops 64 | bytes 512 | tf_op jit(solution)/shard_map/psum | solution.py:40
  71.6 8.8 %psum.53 = f32[64]{0:T(128)S(1)} all-reduce(f32[64]{0:T(128)S(1)} %psum.52), channel_id=1, replica_groups=mesh['gx'=4,'gy'=8] {'gx'}, use_global_device_ids=true, to_apply=%region_9.10 | all-reduce | flops 64 | bytes 512 | tf_op jit(solution)/shard_map/psum | solution.py:41
  80.4 0.1 broadcast_multiply_fusion.1
  80.5 0.1 mul.3122
  80.6 0.1 mul.3148
  80.7 0.1 mul.3178
  80.8 0.1 constant_dynamic-update-slice_fusion.94
  82.2 0.3 select_select_fusion
  82.7 3.9 %collective-permute-start.4 = (f32[5,8,128]{2,1,0:T(8,128)S(1)}, f32[5,8,128]{2,1,0:T(8,128)S(1)}, u32[]{:S(2)}, u32[]{:S(2)}) collective-permute-start(f32[5,8,128]{2,1,0:T(8,128)S(1)} %get-tuple-element.127), channel_id=1, source_target_pairs={{0,8},{8,16},{16,24},{1,9},{9,17},{17,25},{2,10},{10,18},{18,26},{... | collective-permute-start | bytes 61448 | tf_op jit(solution)/shard_map/ppermute | solution.py:47
  86.6 1.9 %collective-permute-start.5 = (f32[5,8,128]{2,1,0:T(8,128)S(1)}, f32[5,8,128]{2,1,0:T(8,128)S(1)}, u32[]{:S(2)}, u32[]{:S(2)}) collective-permute-start(f32[5,8,128]{2,1,0:T(8,128)S(1)} %get-tuple-element.126), channel_id=1, source_target_pairs={{8,0},{16,8},{24,16},{9,1},{17,9},{25,17},{10,2},{18,10},{26,18},{... | collective-permute-start | bytes 61448 | tf_op jit(solution)/shard_map/ppermute | solution.py:47
  88.5 0.6 pad_maximum_fusion.164
  89.1 2.6 %collective-permute-done.5 = f32[5,8,128]{2,1,0:T(8,128)S(1)} collective-permute-done((f32[5,8,128]{2,1,0:T(8,128)S(1)}, f32[5,8,128]{2,1,0:T(8,128)S(1)}, u32[]{:S(2)}, u32[]{:S(2)}) %collective-permute-start.5) | collective-permute-done | bytes 20512 | tf_op jit(solution)/shard_map/ppermute | solution.py:47
  91.9 1.5 %collective-permute-start.6 = (f32[5,10,128]{2,0,1:T(8,128)S(1)}, f32[5,10,128]{2,0,1:T(8,128)S(1)}, u32[]{:S(2)}, u32[]{:S(2)}) collective-permute-start(f32[5,10,128]{2,0,1:T(8,128)S(1)} %stack.172), channel_id=1, source_target_pairs={{0,1},{1,2},{2,3},{3,4},{4,5},{5,6},{6,7},{7,0},{8,9},{9,10},{10,1... | collective-permute-start | bytes 76808 | tf_op jit(solution)/shard_map/ppermute | solution.py:53
  93.7 0.1 slice.1047
  93.8 3.7 %collective-permute-done.6 = f32[5,10,128]{2,0,1:T(8,128)S(1)} collective-permute-done((f32[5,10,128]{2,0,1:T(8,128)S(1)}, f32[5,10,128]{2,0,1:T(8,128)S(1)}, u32[]{:S(2)}, u32[]{:S(2)}) %collective-permute-start.6) | collective-permute-done | bytes 25632 | tf_op jit(solution)/shard_map/ppermute | solution.py:53
  98.4 0.1 constant_dynamic-update-slice_fusion.176
  98.5 0.1 constant_dynamic-update-slice_fusion.175
  98.6 0.1 constant_dynamic-update-slice_fusion.170
  98.7 0.1 constant_dynamic-update-slice_fusion.169
  98.8 0.1 constant_dynamic-update-slice_fusion.168
  98.9 0.1 constant_dynamic-update-slice_fusion.167
  98.9 0.1 constant_dynamic-update-slice_fusion.166
  99.0 0.1 constant_dynamic-update-slice_fusion.165
  99.1 0.1 constant_dynamic-update-slice_fusion.164
  99.2 0.1 constant_dynamic-update-slice_fusion.163
  99.3 0.8 copy-done.3
  (233 shorter events, 6.1 us)
Async XLA Ops:
  0.6 2.0 %copy-start = (f32[19,8,8,128]{3,2,1,0:T(8,128)S(1)}, f32[19,8,8,128]{3,2,1,0:T(8,128)}, u32[]{:S(2)}) copy-start(f32[19,8,8,128]{3,2,1,0:T(8,128)} %param.3) | copy-start | bytes 1867780
  2.6 0.8 copy-start.1
  4.0 0.7 copy-start.2
  35.9 9.0 %collective-permute-start = (f32[5,8,128]{2,1,0:T(8,128)S(1)}, f32[5,8,128]{2,1,0:T(8,128)S(1)}, u32[]{:S(2)}, u32[]{:S(2)}) collective-permute-start(f32[5,8,128]{2,1,0:T(8,128)S(1)} %get-tuple-element.155), channel_id=1, source_target_pairs={{0,8},{8,16},{16,24},{1,9},{9,17},{17,25},{2,10},{10,18},{18,26},{... | collective-permute-start | bytes 61448 | tf_op jit(solution)/shard_map/ppermute | solution.py:47
  39.8 5.1 %collective-permute-start.1 = (f32[5,8,128]{2,1,0:T(8,128)S(1)}, f32[5,8,128]{2,1,0:T(8,128)S(1)}, u32[]{:S(2)}, u32[]{:S(2)}) collective-permute-start(f32[5,8,128]{2,1,0:T(8,128)S(1)} %get-tuple-element.156), channel_id=1, source_target_pairs={{8,0},{16,8},{24,16},{9,1},{17,9},{25,17},{10,2},{18,10},{26,18},{... | collective-permute-start | bytes 61448 | tf_op jit(solution)/shard_map/ppermute | solution.py:47
  45.0 5.6 %collective-permute-start.2 = (f32[5,10,128]{2,0,1:T(8,128)S(1)}, f32[5,10,128]{2,0,1:T(8,128)S(1)}, u32[]{:S(2)}, u32[]{:S(2)}) collective-permute-start(f32[5,10,128]{2,0,1:T(8,128)S(1)} %stack.145), channel_id=1, source_target_pairs={{0,1},{1,2},{2,3},{3,4},{4,5},{5,6},{6,7},{7,0},{8,9},{9,10},{10,1... | collective-permute-start | bytes 76808 | tf_op jit(solution)/shard_map/ppermute | solution.py:53
  45.3 5.5 %collective-permute-start.3 = (f32[5,10,128]{2,0,1:T(8,128)S(1)}, f32[5,10,128]{2,0,1:T(8,128)S(1)}, u32[]{:S(2)}, u32[]{:S(2)}) collective-permute-start(f32[5,10,128]{2,0,1:T(8,128)S(1)} %stack.147), channel_id=1, source_target_pairs={{0,7},{1,0},{2,1},{3,2},{4,3},{5,4},{6,5},{7,6},{8,15},{9,8},{10,9... | collective-permute-start | bytes 76808 | tf_op jit(solution)/shard_map/ppermute | solution.py:53
  82.7 6.4 %collective-permute-start.4 = (f32[5,8,128]{2,1,0:T(8,128)S(1)}, f32[5,8,128]{2,1,0:T(8,128)S(1)}, u32[]{:S(2)}, u32[]{:S(2)}) collective-permute-start(f32[5,8,128]{2,1,0:T(8,128)S(1)} %get-tuple-element.127), channel_id=1, source_target_pairs={{0,8},{8,16},{16,24},{1,9},{9,17},{17,25},{2,10},{10,18},{18,26},{... | collective-permute-start | bytes 61448 | tf_op jit(solution)/shard_map/ppermute | solution.py:47
  86.6 5.1 %collective-permute-start.5 = (f32[5,8,128]{2,1,0:T(8,128)S(1)}, f32[5,8,128]{2,1,0:T(8,128)S(1)}, u32[]{:S(2)}, u32[]{:S(2)}) collective-permute-start(f32[5,8,128]{2,1,0:T(8,128)S(1)} %get-tuple-element.126), channel_id=1, source_target_pairs={{8,0},{16,8},{24,16},{9,1},{17,9},{25,17},{10,2},{18,10},{26,18},{... | collective-permute-start | bytes 61448 | tf_op jit(solution)/shard_map/ppermute | solution.py:47
  91.8 6.2 %collective-permute-start.7 = (f32[5,10,128]{2,0,1:T(8,128)S(1)}, f32[5,10,128]{2,0,1:T(8,128)S(1)}, u32[]{:S(2)}, u32[]{:S(2)}) collective-permute-start(f32[5,10,128]{2,0,1:T(8,128)S(1)} %stack.347), channel_id=1, source_target_pairs={{0,7},{1,0},{2,1},{3,2},{4,3},{5,4},{6,5},{7,6},{8,15},{9,8},{10,9... | collective-permute-start | bytes 76808 | tf_op jit(solution)/shard_map/ppermute | solution.py:53
  91.9 5.6 %collective-permute-start.6 = (f32[5,10,128]{2,0,1:T(8,128)S(1)}, f32[5,10,128]{2,0,1:T(8,128)S(1)}, u32[]{:S(2)}, u32[]{:S(2)}) collective-permute-start(f32[5,10,128]{2,0,1:T(8,128)S(1)} %stack.172), channel_id=1, source_target_pairs={{0,1},{1,2},{2,3},{3,4},{4,5},{5,6},{6,7},{7,0},{8,9},{9,10},{10,1... | collective-permute-start | bytes 76808 | tf_op jit(solution)/shard_map/ppermute | solution.py:53
  99.3 0.8 copy-start.3
